TPU v7x, 128 devices: a 2x2x16 block of a 8x8x16 slice. The times are simulated.
128 devices in a mesh: groups: 4 (over x, y), traces: 32 (over z, core).
Axes of the slice: x: 2, y: 2, z: 16, core: 2. Of those that a mesh axis runs over, the one named last changes fastest.
The devices are a block of a 8x8x16 slice.
Arguments:
- raw_traces: float32 [32768, 8192], P(('groups', 'traces')), parts along dimension 0, may hold values from -6 to 6
- filter_index: int32 [32768], P(('groups', 'traces')), parts along dimension 0, may hold values from 0 to 255
- channel_order: int32 [1024], P('groups'), parts along dimension 0, may hold values from 0 to 255, each once
- wavelets: float32 [256, 256], P('traces'), may hold values from -0.375 to 0.375
- damping: float32 [256], P('traces'), may hold values from 0.02 to 0.5
Outputs:
- deconvolved: float32 [32768, 8192], P(('groups', 'traces')), parts along dimension 0
There are 4 independent parts, one for each index of `groups`. A program takes and returns all parts, laid end to end along the dimension named above; an argument that names none is the same for every part. Nothing has to cross between parts.
Inputs may be any that keep to these rules, and one draw needn't show every extreme that they name: `channel_order`: each of 0 to 255 appears once.
All inputs are finite; a program needn't handle non-finite values.
Results may differ from a plain program's by a relative error of at most 0.00021.
Values sent between devices are 32-bit elements; how exact they have to be, the bound alone decides.
A program may use at most 192 MiB of HBM per device.

v0:
```python
import math

import jax
import jax.numpy as jnp
from jax import lax
from jax.sharding import PartitionSpec as P

P_SIZE = 64


HIGHEST = lax.Precision.HIGHEST


def in_one_piece(arrays, axis, dim, along):
    both = jnp.concatenate(arrays, axis=along)
    out, at, gathered = (lax.all_gather(both, axis, axis=dim, tiled=True), 0, [])
    for a in arrays:
        gathered.append(lax.slice_in_dim(out, at, at + a.shape[along], axis=along))
        at += a.shape[along]
    return tuple(gathered)


def angle_table(height, across, period, orient):
    row_ids = lax.broadcasted_iota(jnp.int32, (height, across), 0)
    col_ids = lax.broadcasted_iota(jnp.int32, (height, across), 1)
    phases = (row_ids * col_ids % period).astype(jnp.float32) * (2.0 * math.pi / period)
    return (jnp.cos(phases), orient * jnp.sin(phases))


def forward_spectra(signal, factor):
    traces_here, length = signal.shape
    second = length // factor
    blocks = signal.reshape(traces_here, factor, second)
    cos_p, sin_p = angle_table(factor, factor, factor, -1.0)
    first_re = jnp.einsum("tnq,nk->tkq", blocks, cos_p, precision=HIGHEST)
    first_im = jnp.einsum("tnq,nk->tkq", blocks, sin_p, precision=HIGHEST)
    twist_c, twist_s = angle_table(factor, second, length, -1.0)
    mid_re = first_re * twist_c - first_im * twist_s
    mid_im = first_re * twist_s + first_im * twist_c
    cos_q, sin_q = angle_table(second, second, second, -1.0)
    out_re = jnp.einsum("tkq,qm->tkm", mid_re, cos_q, precision=HIGHEST) - jnp.einsum(
        "tkq,qm->tkm", mid_im, sin_q, precision=HIGHEST
    )
    out_im = jnp.einsum("tkq,qm->tkm", mid_re, sin_q, precision=HIGHEST) + jnp.einsum(
        "tkq,qm->tkm", mid_im, cos_q, precision=HIGHEST
    )
    return (out_re, out_im)


def inverse_signal(spec_re, spec_im):
    traces_here, factor, second = spec_re.shape
    length = factor * second
    cos_q, sin_q = angle_table(second, second, second, 1.0)
    back_re = jnp.einsum("tkm,mq->tkq", spec_re, cos_q, precision=HIGHEST) - jnp.einsum(
        "tkm,mq->tkq", spec_im, sin_q, precision=HIGHEST
    )
    back_im = jnp.einsum("tkm,mq->tkq", spec_re, sin_q, precision=HIGHEST) + jnp.einsum(
        "tkm,mq->tkq", spec_im, cos_q, precision=HIGHEST
    )
    twist_c, twist_s = angle_table(factor, second, length, 1.0)
    turned_re = back_re * twist_c - back_im * twist_s
    turned_im = back_re * twist_s + back_im * twist_c
    cos_p, sin_p = angle_table(factor, factor, factor, 1.0)
    signal = jnp.einsum("tkq,kn->tnq", turned_re, cos_p, precision=HIGHEST) - jnp.einsum(
        "tkq,kn->tnq", turned_im, sin_p, precision=HIGHEST
    )
    return (signal / length).reshape(traces_here, length)


def gains_from(wavelets, damping, length):
    padded = jnp.pad(wavelets, ((0, 0), (0, length - wavelets.shape[1])))
    spec_re, spec_im = forward_spectra(padded, P_SIZE)
    power = spec_re * spec_re + spec_im * spec_im
    level = jnp.mean(power, axis=(1, 2), keepdims=True)
    denom = power + damping[:, None, None] * (level + 1e-06)
    return (spec_re / denom, -spec_im / denom)


def local(raw_traces, filter_index, channel_order, wavelets, damping):
    length = raw_traces.shape[1]
    own_re, own_im = gains_from(wavelets, damping, length)
    gain_re, gain_im = in_one_piece((own_re, own_im), "traces", 0, 1)
    spec_re, spec_im = forward_spectra(raw_traces, P_SIZE)
    pick_re = jnp.take(gain_re, filter_index, axis=0)
    pick_im = jnp.take(gain_im, filter_index, axis=0)
    out_re = spec_re * pick_re - spec_im * pick_im
    out_im = spec_re * pick_im + spec_im * pick_re
    result = inverse_signal(out_re, out_im)
    groups_n = lax.axis_size("traces")
    rows_here = result.shape[0]
    stacked = result.reshape(groups_n, rows_here // groups_n, 1, length)
    moved = lax.all_to_all(stacked, "traces", split_axis=0, concat_axis=2, tiled=True)
    ordered = moved.reshape(rows_here, length)
    return jnp.take(ordered, channel_order, axis=0)


def solution(mesh):
    placed = (
        P(("groups", "traces"), None),
        P(("groups", "traces")),
        P("groups"),
        P("traces", None),
        P("traces"),
    )
    return jax.shard_map(
        local, mesh=mesh, in_specs=placed, out_specs=P(("groups", "traces"), None), check_vma=False
    )
```

profile of v0, /device:TPU:69, one launch (start us, length us, event | category | flops | bytes accessed | tf_op | source)
XLA Modules:
  0.0 691.3 jit_solution(12578228415490859509)
XLA Ops:
  6.5 0.0 all-gather.2.cloned.1.call-start
  6.6 0.1 broadcast_multiply_fusion
  6.7 0.7 pad_bitcast_fusion
  7.4 0.5 fusion.14
  8.0 0.5 fusion.16
  8.5 0.6 fusion.20
  9.1 0.6 fusion.22
  9.7 0.6 convolution_subtract_fusion
  10.4 0.7 fusion.26
  11.1 0.7 add_multiply_fusion
  11.7 0.1 add_divide_fusion
  11.9 0.8 pad_maximum_fusion
  12.7 0.1 all-gather.2.cloned.1.call-update
  12.8 0.0 copy-start.3
  12.8 5.0 copy.32
  17.8 0.0 copy-done.3
  17.8 0.0 copy-start.1
  17.8 0.1 fusion.95
  18.0 3.1 copy-done.1
  21.1 10.0 %fusion.61 = f32[64,256,128]{2,0,1:T(8,128)} fusion(f32[256,64,128]{2,1,0:T(8,128)S(1)} %bitcast.93), kind=kOutput, calls=%fused_computation.90 | convolution fusion | flops 1610674176 | bytes 16777216 | tf_op jit(solution)/shard_map/tnq,nk->tkq/dot_general | solution.py:36
  31.1 13.9 %add_bitcast_fusion = (f32[256,64,128]{2,1,0:T(8,128)S(1)}, f32[256,64,128]{2,1,0:T(8,128)S(1)}) fusion(f32[64,256,128]{2,0,1:T(8,128)} %fusion.61, f32[64,128]{1,0:T(8,128)S(1)} %get-tuple-element.18, f32[64,128]{1,0:T(8,128)S(1)} %get-tuple-element.19, f32[256,64,128]{2,1,0:T(8,128)} %bitcast.94), kind=kOutput, calls=%fused_computation.14 | convolution fusion | flops 1623252992 | bytes 33619968 | tf_op jit(solution)/shard_map/tnq,nk->tkq/dot_general | solution.py:35
  45.0 0.0 copy-start
  45.0 15.9 %fusion.4 = f32[256,64,128]{2,0,1:T(8,128)} fusion(f32[256,64,128]{2,1,0:T(8,128)S(1)} %get-tuple-element.10), kind=kOutput, calls=%fused_computation.16 | convolution fusion | flops 3221454848 | bytes 16777216 | tf_op jit(solution)/shard_map/tkq,qm->tkm/dot_general | solution.py:44
  60.9 16.0 %fusion.6 = f32[256,64,128]{2,0,1:T(8,128)} fusion(f32[256,64,128]{2,1,0:T(8,128)S(1)} %get-tuple-element.10), kind=kOutput, calls=%fused_computation.18 | convolution fusion | flops 3221471232 | bytes 16777216 | tf_op jit(solution)/shard_map/tkq,qm->tkm/dot_general | solution.py:41
  76.9 0.0 copy-done
  76.9 15.7 %fusion.10 = f32[256,64,128]{2,0,1:T(8,128)} fusion(f32[256,64,128]{2,1,0:T(8,128)S(1)} %get-tuple-element.11), kind=kOutput, calls=%fused_computation.22 | convolution fusion | flops 3221454848 | bytes 16777216 | tf_op jit(solution)/shard_map/tkq,qm->tkm/dot_general | solution.py:41
  92.6 30.7 %all-gather.2.cloned.1.call-done = f32[256,128,128]{2,1,0:T(8,128)} async-done(((f32[8,128,128]{2,1,0:T(8,128)}), f32[256,128,128]{2,1,0:T(8,128)}) %all-gather.2.cloned.1.call-update) | async-done | bytes 16777232 | tf_op jit(solution)/shard_map/all_gather | solution.py:16
  123.3 11.0 %fusion.183 = (f32[256,64,128]{2,1,0:T(8,128)}, f32[256,64,128]{2,1,0:T(8,128)}) fusion(f32[256,128,128]{2,1,0:T(8,128)} %all-gather.2.cloned.1.call-done), kind=kLoop, calls=%fused_computation.202 | loop fusion | bytes 33554432 | tf_op jit(solution)/shard_map/slice | solution.py:18
  134.3 7.7 %gather_fusion.2 = f32[256,64,128]{2,1,0:T(8,128)} fusion(f32[256,64,128]{2,1,0:T(8,128)} %get-tuple-element.12, s32[1024]{0:T(1024)S(1)} %pad_clamp_fusion.1), kind=kCustom, calls=%fused_computation.1.clone | custom fusion | bytes 16778240 | tf_op jit(solution)/shard_map/jit(_take)/gather | solution.py:85
  142.0 7.9 %gather_fusion.1 = f32[256,64,128]{2,1,0:T(8,128)} fusion(f32[256,64,128]{2,1,0:T(8,128)} %get-tuple-element.13, s32[1024]{0:T(1024)S(1)} %pad_clamp_fusion.1), kind=kCustom, calls=%fused_computation.clone | custom fusion | bytes 16778240 | tf_op jit(solution)/shard_map/jit(_take)/gather | solution.py:84
  149.9 38.7 %multiply_add_fusion.1 = (f32[256,64,128]{2,0,1:T(8,128)}, f32[256,64,128]{2,0,1:T(8,128)}) fusion(f32[256,64,128]{2,1,0:T(8,128)} %gather_fusion.1, f32[256,64,128]{2,1,0:T(8,128)} %gather_fusion.2, pred[256]{0:T(512)(128)(4,1)S(1)} %compare_and_fusion, f32[256,64,128]{2,0,1:T(8,128)} %fusion.4, f32[256,64,128]{2,0,1:T(8,128)} %fusion.10, ...), kind=kOutput, calls=%fused_computation.12 | convolution fusion | flops 3242442752 | bytes 67109120 | tf_op jit(solution)/shard_map/tkq,qm->tkm/dot_general | solution.py:44
  188.6 0.0 slice-start
  188.6 0.0 slice-start.1
  188.6 0.0 slice-start.2
  188.6 12.7 %fusion.38 = f32[256,64,128]{2,0,1:T(8,128)} fusion(f32[256,64,128]{2,0,1:T(8,128)} %get-tuple-element.6), kind=kOutput, calls=%fused_computation.61 | convolution fusion | flops 3221454848 | bytes 16777216 | tf_op jit(solution)/shard_map/tkm,mq->tkq/dot_general | solution.py:57
  201.2 0.0 slice-done
  201.2 0.0 slice-done.1
  201.2 0.0 slice-start.3
  201.2 9.4 %fusion.32 = f32[256,64,128]{2,0,1:T(8,128)} fusion(f32[256,64,128]{2,0,1:T(8,128)S(1)} %bitcast.90), kind=kOutput, calls=%fused_computation.55 | convolution fusion | flops 3221454848 | bytes 16777216 | tf_op jit(solution)/shard_map/tkm,mq->tkq/dot_general | solution.py:54
  210.6 0.0 slice-done.2
  210.6 0.0 slice-done.3
  210.6 9.3 %fusion.40 = f32[256,64,128]{2,0,1:T(8,128)} fusion(f32[256,64,128]{2,0,1:T(8,128)S(1)} %bitcast.92), kind=kOutput, calls=%fused_computation.63 | convolution fusion | flops 3221454848 | bytes 16777216 | tf_op jit(solution)/shard_map/tkm,mq->tkq/dot_general | solution.py:54
  219.9 18.5 %multiply_subtract_fusion = (f32[256,64,128]{2,0,1:T(8,128)}, f32[256,64,128]{2,0,1:T(8,128)}) fusion(f32[64,128]{1,0:T(8,128)S(1)} %fusion.95, f32[64,128]{1,0:T(8,128)S(1)} %get-tuple-element.19, f32[256,64,128]{2,0,1:T(8,128)} %fusion.38, f32[256,64,128]{2,0,1:T(8,128)} %fusion.40, f32[256,64,128]{2,0,1:T(8,128)} %fusion.32, ...), kind=kOutput, calls=%fused_computation.11 | convolution fusion | flops 3238232064 | bytes 50397184 | tf_op jit(solution)/shard_map/tkm,mq->tkq/dot_general | solution.py:57
  238.5 0.0 copy-start.2
  238.5 15.6 %fusion = f32[64,256,128]{2,0,1:T(8,128)S(1)} fusion(f32[256,64,128]{2,0,1:T(8,128)} %get-tuple-element.9), kind=kOutput, calls=%fused_computation.3 | convolution fusion | flops 1610670080 | bytes 16777216 | tf_op jit(solution)/shard_map/tkq,kn->tnq/dot_general | solution.py:64
  254.1 0.0 copy-done.2
  254.1 17.5 %multiply_bitcast_fusion = f32[256,64,128]{2,1,0:T(8,128)} fusion(f32[64,256,128]{2,0,1:T(8,128)S(1)} %fusion, f32[256,64,128]{2,0,1:T(8,128)S(1)} %copy-done.2), kind=kOutput, calls=%fused_computation.9 | convolution fusion | flops 1614864384 | bytes 25165824 | tf_op jit(solution)/shard_map/tkq,kn->tnq/dot_general | solution.py:64
  271.7 9.4 %reshape_reshape.3 = f32[32,8,1,8192]{3,1,0,2:T(8,128)} reshape(f32[256,64,128]{2,1,0:T(8,128)} %multiply_bitcast_fusion) | data formatting | bytes 16777216 | tf_op jit(solution)/shard_map/reshape;reshape | solution.py:91
  281.0 0.0 copy-start.4
  281.0 10.1 %all-to-all-start = ((f32[32,8,1,8192]{3,1,2,0:T(8,128)}), f32[32,8,1,8192]{3,1,2,0:T(8,128)}, u32[]{:S(2)}, u32[]{:S(2)}) async-start(f32[32,8,1,8192]{3,1,2,0:T(8,128)} %bitcast.95), calls=%async_computation | async-start | bytes 16777216 | tf_op jit(solution)/shard_map/all_to_all | solution.py:92
  291.1 0.0 copy-done.4
  291.2 360.0 %all-to-all-done = f32[32,8,1,8192]{3,1,2,0:T(8,128)} async-done(((f32[32,8,1,8192]{3,1,2,0:T(8,128)}), f32[32,8,1,8192]{3,1,2,0:T(8,128)}, u32[]{:S(2)}, u32[]{:S(2)}) %all-to-all-start) | async-done | bytes 8388640 | tf_op jit(solution)/shard_map/all_to_all | solution.py:92
  651.2 11.6 %copy.31 = f32[1,8,32,1,8192]{4,2,1,3,0:T(8,128)} copy(f32[1,8,32,1,8192]{4,1,2,3,0:T(8,128)} %bitcast.13) | data formatting | bytes 16777216 | tf_op jit(solution)/shard_map/all_to_all | solution.py:92
  662.8 13.2 %gather_fusion = f32[256,8192]{1,0:T(8,128)} fusion(f32[256,8192]{1,0:T(8,128)} %bitcast.88, s32[1024]{0:T(1024)S(1)} %pad_clamp_fusion), kind=kCustom, calls=%fused_computation.2 | custom fusion | bytes 16778240 | tf_op jit(solution)/shard_map/jit(_take)/gather | solution.py:94
  676.0 8.0 %broadcast_select_fusion = f32[256,8192]{1,0:T(8,128)} fusion(f32[256,8192]{1,0:T(8,128)} %gather_fusion, pred[256]{0:T(512)(128)(4,1)S(1)} %compare_and_fusion.1), kind=kLoop, calls=%fused_computation.24 | loop fusion | flops 2097152 | bytes 16777472 | tf_op jit(solution)/shard_map/jit(_take)/select_n | solution.py:94
  (8 shorter events, 0.0 us)
Async XLA Ops:
  6.5 116.7 %all-gather.2.cloned.1.call-start = ((), (), s32[]{:S(2)}) async-start(), calls=%async_computation.1 | async-start | bytes 17301504 | tf_op jit(solution)/shard_map/all_gather | solution.py:16
  12.8 5.0 copy-start.3
  17.8 3.3 copy-start.1
  45.0 31.9 %copy-start = (f32[256,64,128]{2,1,0:T(8,128)}, f32[256,64,128]{2,1,0:T(8,128)S(1)}, u32[]{:S(2)}) copy-start(f32[256,64,128]{2,1,0:T(8,128)S(1)} %get-tuple-element.11) | copy-start | bytes 25165828
  188.6 12.7 %slice-start = ((s8[8388608]{0:T(1024)(128)(4,1)}), s8[4194304]{0:T(1024)(128)(4,1)S(1)}, s32[]{:S(2)}) async-start(s8[8388608]{0:T(1024)(128)(4,1)} %bitcast.89), calls=%async_computation.2 | async-start | bytes 8388608
  188.6 12.7 %slice-start.1 = ((s8[8388608]{0:T(1024)(128)(4,1)}), s8[4194304]{0:T(1024)(128)(4,1)S(1)}, s32[]{:S(2)}) async-start(s8[8388608]{0:T(1024)(128)(4,1)} %bitcast.89), calls=%async_computation.3 | async-start | bytes 8388608
  188.6 22.0 %slice-start.2 = ((s8[8388608]{0:T(1024)(128)(4,1)}), s8[4194304]{0:T(1024)(128)(4,1)S(1)}, s32[]{:S(2)}) async-start(s8[8388608]{0:T(1024)(128)(4,1)} %bitcast.91), calls=%async_computation.4 | async-start | bytes 8388608
  201.2 9.4 %slice-start.3 = ((s8[8388608]{0:T(1024)(128)(4,1)}), s8[4194304]{0:T(1024)(128)(4,1)S(1)}, s32[]{:S(2)}) async-start(s8[8388608]{0:T(1024)(128)(4,1)} %bitcast.91), calls=%async_computation.5 | async-start | bytes 8388608
  238.5 15.6 %copy-start.2 = (f32[256,64,128]{2,0,1:T(8,128)S(1)}, f32[256,64,128]{2,0,1:T(8,128)}, u32[]{:S(2)}) copy-start(f32[256,64,128]{2,0,1:T(8,128)} %get-tuple-element.8) | copy-start | bytes 25165828
  281.0 10.1 %copy-start.4 = (s32[256]{0:T(256)S(1)}, s32[256]{0:T(256)}, u32[]{:S(2)}) copy-start(s32[256]{0:T(256)} %param.9) | copy-start | bytes 3076
  281.0 370.1 %all-to-all-start = ((f32[32,8,1,8192]{3,1,2,0:T(8,128)}), f32[32,8,1,8192]{3,1,2,0:T(8,128)}, u32[]{:S(2)}, u32[]{:S(2)}) async-start(f32[32,8,1,8192]{3,1,2,0:T(8,128)} %bitcast.95), calls=%async_computation | async-start | bytes 16777216 | tf_op jit(solution)/shard_map/all_to_all | solution.py:92
Sparse Core Ops, SparseCore 0:
  12.9 110.3 all-gather.1
where the time goes:
time: 704 us; the launch traced here: 691 us
  waiting for transfers between devices  391 us (56%)
  matrix products  197 us (28%)
  local copies, waits for them, and re-layouts  69.7 us (10%)
  between operations  14.1 us (2%)
  starting transfers between devices  10.1 us (1%)
  other arithmetic  9.91 us (1%)
    all_to_all x1, waiting for transfers between devices, local(): lax.all_to_all(stacked, 'traces', split_axis=0, concat_axis=2, tiled=True)  360 us
    dot_general x2, matrix products, forward_spectra(): jnp.einsum('tkq,qm->tkm', mid_re, sin_q, precision=HIGHEST)  39.3 us
    all_gather x1, waiting for transfers between devices, in_one_piece(): lax.all_gather(both, axis, axis=dim, tiled=True)  30.7 us
    dot_general x1, matrix products, inverse_signal(): jnp.einsum('tkm,mq->tkq', spec_re, sin_q, precision=HIGHEST)  18.5 us
    dot_general x1, matrix products, inverse_signal(): jnp.einsum('tkq,kn->tnq', turned_re, cos_p, precision=HIGHEST)  17.5 us
    dot_general x2, matrix products, forward_spectra(): jnp.einsum('tkq,qm->tkm', mid_im, sin_q, precision=HIGHEST)  16.6 us
    dot_general x2, matrix products, forward_spectra(): jnp.einsum('tkq,qm->tkm', mid_im, cos_q, precision=HIGHEST)  16.6 us
    dot_general x2, matrix products, forward_spectra(): jnp.einsum('tkq,qm->tkm', mid_re, cos_q, precision=HIGHEST)  16.3 us
  transfers between devices with their start and end apart: 2, of which 2 were waited for; matrix products, arithmetic and copies ran while one was open for 11% of the time, Pallas kernels for 0%

commit v1 on v0

v1 whole, which is shorter than its diff:
```python
import functools
import math

import jax
import jax.numpy as jnp
import numpy as np
from jax import lax
from jax.experimental import pallas as pl
from jax.experimental.pallas import tpu as pltpu
from jax.sharding import PartitionSpec as P

MESH = pl.DeviceIdType.MESH
HIGHEST = lax.Precision.HIGHEST
HALF_ROOT = math.sqrt(0.5)

KEPT = [a + 8 * b for a in (1, 2, 3) for b in range(8)] + [8 * b for b in range(5)] + [4 + 8 * b for b in range(4)]
NK = len(KEPT)
CHUNK = 11
PITCH = 65
VMEM_LIMIT = 34 * 2**20


def tables():
    q = np.arange(128)
    turn = 2.0 * np.pi * (np.outer(q, q) % 128) / 128
    c, s = np.cos(turn), np.sin(turn)
    across = np.block([[c, -s], [s, c]]).astype(np.float32)
    twist = []
    for shift in (0, 128):
        angle = 2.0 * np.pi * (np.outer(KEPT, q + shift) % 8192) / 8192
        twist += [np.cos(angle), -np.sin(angle)]
    twist = np.stack(twist).astype(np.float32)
    return across, np.ascontiguousarray(np.broadcast_to(twist[:, :, None, :], (4, NK, 8, 128)))


def rotate(re, im, step):
    step %= 64
    if step == 0:
        return re, im
    c, s = math.cos(2 * math.pi * step / 64), math.sin(2 * math.pi * step / 64)
    return re * c + im * s, im * c - re * s


def four(x):
    (ar, ai), (br, bi), (cr, ci), (dr, di) = x
    sr, si, tr, ti = ar + cr, ai + ci, ar - cr, ai - ci
    ur, ui, vr, vi = br + dr, bi + di, br - dr, bi - di
    return [(sr + ur, si + ui), (tr + vi, ti - vr), (sr - ur, si - ui), (tr - vi, ti + vr)]


def eight(x):
    e, o = four(x[0::2]), four(x[1::2])
    r = HALF_ROOT
    w = [
        o[0],
        (r * (o[1][0] + o[1][1]), r * (o[1][1] - o[1][0])),
        (o[2][1], -o[2][0]),
        (r * (o[3][1] - o[3][0]), -r * (o[3][0] + o[3][1])),
    ]
    low = [(e[k][0] + w[k][0], e[k][1] + w[k][1]) for k in range(4)]
    high = [(e[k][0] - w[k][0], e[k][1] - w[k][1]) for k in range(4)]
    return low + high


def eight_real(x):
    s, t, u, v = x[0] + x[4], x[0] - x[4], x[2] + x[6], x[2] - x[6]
    s2, t2, u2, v2 = x[1] + x[5], x[1] - x[5], x[3] + x[7], x[3] - x[7]
    e0, o0 = s + u, s2 + u2
    wr, wi = HALF_ROOT * (t2 - v2), -HALF_ROOT * (t2 + v2)
    return [
        (e0 + o0, None),
        (t + wr, wi - v),
        (s - u, u2 - s2),
        (t - wr, v + wi),
        (e0 - o0, None),
    ]


def total(terms):
    terms = list(terms)
    while len(terms) > 1:
        terms = [terms[i] + terms[i + 1] if i + 1 < len(terms) else terms[i] for i in range(0, len(terms), 2)]
    return terms[0]


def rows_forward(x_ref, part, lhs):
    for b in range(8):
        v = eight_real([x_ref[:, pl.ds((8 * a + b) * 128, 128)] for a in range(8)])
        part[b, 0] = v[0][0]
        part[b, 7] = v[4][0]
        for k in (1, 2, 3):
            re, im = rotate(v[k][0], v[k][1], b * k)
            part[b, 2 * k - 1] = re
            part[b, 2 * k] = im
    for k in (1, 2, 3):
        out = eight([(part[b, 2 * k - 1], part[b, 2 * k]) for b in range(8)])
        for b in range(8):
            lhs[8 * (k - 1) + b, :, 0:128] = out[b][0]
            lhs[8 * (k - 1) + b, :, 128:256] = out[b][1]
    out = eight_real([part[b, 0] for b in range(8)])
    for b in range(5):
        lhs[24 + b, :, 0:128] = out[b][0]
        lhs[24 + b, :, 128:256] = jnp.zeros((8, 128), jnp.float32) if out[b][1] is None else out[b][1]
    real = [part[b, 7] for b in range(8)]
    for j in range(4):
        angles = [2 * math.pi * b * (2 * j + 1) / 16 for b in range(8)]
        lhs[29 + j, :, 0:128] = total(real[b] * math.cos(angles[b]) for b in range(8))
        lhs[29 + j, :, 128:256] = total(real[b] * -math.sin(angles[b]) for b in range(1, 8))


def rows_inverse(spec, part, out_ref):
    def at(i):
        return spec[i, :, 0:128], spec[i, :, 128:256]

    for k in (1, 2, 3):
        out = eight([at(8 * (k - 1) + b) for b in range(8)])
        for b in range(8):
            re, im = rotate(out[b][0], out[b][1], b * k)
            part[b, 2 * k - 1] = re
            part[b, 2 * k] = im
    zero = [at(24 + j) for j in range(5)]
    four_ = [at(29 + j) for j in range(4)]
    for b in range(8):
        terms = [zero[0][0], zero[4][0] if b % 2 == 0 else -zero[4][0]]
        for j in (1, 2, 3):
            terms.append(rotate(*zero[j], 8 * b * j)[0])
        part[b, 0] = total(terms)
        part[b, 7] = total(rotate(*four_[j], b * (4 + 8 * j))[0] for j in range(4))
    for b in range(8):
        e0, p1, m1, p2, m2, p3, m3, e4 = (part[b, i] for i in range(8))
        g0, g1 = e0 + e4, e0 - e4
        for a, base, turn in (
            (0, g0 + p2, p1 + p3),
            (2, g0 - p2, m1 - m3),
            (1, g1 + m2, HALF_ROOT * ((p1 + m1) + (m3 - p3))),
            (3, g1 - m2, HALF_ROOT * ((m1 - p1) + (p3 + m3))),
        ):
            out_ref[pl.ds(8 * a + b, 8, stride=PITCH), :] = base + turn
            out_ref[pl.ds(8 * (a + 4) + b, 8, stride=PITCH), :] = base - turn


def deconvolve(x_ref, out_ref, tap_ref, floor_ref, across, twist, part, lhs, spec):
    rows_forward(x_ref, part, lhs)
    h0, h1 = tap_ref[:, 0:128][None], tap_ref[:, 128:256][None]
    for at in range(0, NK, CHUNK):
        here = pl.ds(at, CHUNK)
        c, s = twist[0, here], twist[1, here]
        re, im = lhs[here, :, 0:128], lhs[here, :, 128:256]
        lhs[here, :, 0:128] = re * c - im * s
        lhs[here, :, 128:256] = re * s + im * c
        there = pl.ds(NK + at, CHUNK)
        lhs[there, :, 0:128] = h0 * c + h1 * twist[2, here]
        lhs[there, :, 128:256] = h0 * s + h1 * twist[3, here]
    both = jnp.dot(lhs[...].reshape(2 * NK * 8, 256), across[...], precision=HIGHEST, preferred_element_type=jnp.float32)
    spec[...] = both.reshape(2 * NK, 8, 256)
    floor = floor_ref[...][None]
    for at in range(0, NK, CHUNK):
        here, there = pl.ds(at, CHUNK), pl.ds(NK + at, CHUNK)
        xr, xi = spec[here, :, 0:128], spec[here, :, 128:256]
        hr, hi = spec[there, :, 0:128], spec[there, :, 128:256]
        scale = (2.0 / 8192) / ((hr * hr + hi * hi) + floor)
        lhs[here, :, 0:128] = (xr * hr + xi * hi) * scale
        lhs[here, :, 128:256] = (xr * hi - xi * hr) * scale
    back = jnp.dot(
        lhs[pl.ds(0, NK)].reshape(NK * 8, 256), across[...], precision=HIGHEST, preferred_element_type=jnp.float32
    )
    spec[pl.ds(0, NK)] = back.reshape(NK, 8, 256)
    for at in range(0, NK, CHUNK):
        here = pl.ds(at, CHUNK)
        c, s = twist[0, here], twist[1, here]
        re, im = spec[here, :, 0:128], spec[here, :, 128:256]
        spec[here, :, 0:128] = re * c - im * s
        spec[here, :, 128:256] = re * s + im * c
    for i in (24, 28):
        spec[i] = spec[i] * 0.5
    rows_inverse(spec, part, out_ref)


def exchange_kernel(
    n,
    x_ref, index_ref, damp_ref, wave_ref, across_ref, twist_ref,
    o_ref,
    raw, own, note, bank, taps, floors, across, twist, part, lhs, spec,
    send, recv, note_send, note_recv, wave_send, wave_recv, fours_send, fours_recv, pass_sem, own_sem, table_sem,
):
    me = lax.axis_index("traces")
    chips = n // 2
    z, core = me // 2, me % 2

    def place_of(z, core):
        return core * chips + (z % 4) * (chips // 4) + z // 4

    mine = place_of(z, core)

    def offset(k):
        later = (k + n - 4) // n
        dz = later * ((chips // 2 - k // 4) * (1 - 2 * (k % 2))) + (1 - later) * (chips // 2) * (k // 2)
        dc = later * ((k // 2) % 2) + (1 - later) * (k % 2)
        return dz, dc

    def target(k):
        dz, dc = offset(k)
        return ((z + dz + chips) % chips) * 2 + (core + dc) % 2

    def source(k):
        dz, dc = offset(k)
        return (z - dz + chips) % chips, (core + dc) % 2

    def eight_rows(i):
        return pl.ds(pl.multiple_of(i * 8, 8), 8)

    def raw_copy(k):
        t = target(k)
        return pltpu.make_async_remote_copy(
            src_ref=x_ref.at[eight_rows(t)], dst_ref=raw.at[k], send_sem=send.at[k], recv_sem=recv.at[k],
            device_id={"traces": t}, device_id_type=MESH,
        )

    def note_copy(k):
        t = target(k)
        return pltpu.make_async_remote_copy(
            src_ref=own.at[t], dst_ref=note.at[mine], send_sem=note_send.at[k], recv_sem=note_recv.at[k],
            device_id={"traces": t}, device_id_type=MESH,
        )

    def wave_copy(j):
        return pltpu.make_async_remote_copy(
            src_ref=wave_ref, dst_ref=bank.at[core, z % 4, z // 4], send_sem=wave_send.at[j], recv_sem=wave_recv.at[j],
            device_id={"traces": ((z + 4 * j) % chips) * 2 + core}, device_id_type=MESH,
        )

    def fours_copy(j):
        away = (0, 1, 2, chips - 1)[j]
        return pltpu.make_async_remote_copy(
            src_ref=bank.at[core, z % 4], dst_ref=bank.at[core, z % 4], send_sem=fours_send.at[j], recv_sem=fours_recv.at[j],
            device_id={"traces": ((z + away) % chips) * 2 + core}, device_id_type=MESH,
        )

    def pass_copy():
        return pltpu.make_async_remote_copy(
            src_ref=bank.at[core], dst_ref=bank.at[core], send_sem=pass_sem.at[0], recv_sem=pass_sem.at[1],
            device_id={"traces": z * 2 + 1 - core}, device_id_type=MESH,
        )

    barrier = pltpu.get_barrier_semaphore()

    def greet(k, _):
        pl.semaphore_signal(barrier, inc=1, device_id={"traces": target(k)}, device_id_type=MESH)
        return 0

    lax.fori_loop(1, n, greet, 0)
    own_copy = pltpu.make_async_copy(x_ref.at[eight_rows(me)], raw.at[0], own_sem)
    own_copy.start()
    across_copy = pltpu.make_async_copy(across_ref, across, table_sem.at[0])
    across_copy.start()
    twist_copy = pltpu.make_async_copy(twist_ref, twist, table_sem.at[1])
    twist_copy.start()
    bank[core, z % 4, z // 4] = wave_ref[...]
    lane = lax.broadcasted_iota(jnp.int32, (1, 128), 1)
    damp = jnp.zeros((1, 128), jnp.float32)
    for i in range(8):
        damp = jnp.where(lane == 8 + i, damp_ref[i], damp)

    def fill(e, _):
        row = damp
        for i in range(8):
            row = jnp.where(lane == i, index_ref[e * 8 + i].astype(jnp.float32), row)
        own[e] = row
        return 0

    lax.fori_loop(0, n, fill, 0)
    note[mine] = own[me]
    pl.semaphore_wait(barrier, n - 1)

    def start_note(k, _):
        note_copy(k).start()
        return 0

    def start_wave(j, _):
        wave_copy(j).start()
        return 0

    def start_raw(k, _):
        raw_copy(k).start()
        return 0

    def wait_wave(j, _):
        wave_copy(j).wait()
        return 0

    def wait_note(k, _):
        note_copy(k).wait()
        return 0

    lax.fori_loop(1, chips // 4, start_wave, 0)
    lax.fori_loop(1, n, start_note, 0)
    lax.fori_loop(1, 8, start_raw, 0)
    own_copy.wait()
    across_copy.wait()
    twist_copy.wait()
    lax.fori_loop(1, chips // 4, wait_wave, 0)
    for j in (1, 2, 3):
        fours_copy(j).start()
    lax.fori_loop(8, n, start_raw, 0)
    for j in (1, 2, 3):
        fours_copy(j).wait()
    pass_copy().start()
    lax.fori_loop(1, n, wait_note, 0)
    pass_copy().wait()

    notes = note[...]
    lanes = lax.broadcasted_iota(jnp.int32, (n, 8, 128), 2)
    place = lax.broadcasted_iota(jnp.int32, (n, 8, 128), 1)
    wanted = jnp.sum(jnp.where(lanes == place, notes, 0.0), axis=2, keepdims=True).reshape(8 * n, 1)
    damping = jnp.sum(jnp.where(lanes == place + 8, notes, 0.0), axis=2, keepdims=True).reshape(8 * n, 1)
    every = bank[...].reshape(8 * n, 256)
    level = jnp.sum(every * every, axis=1, keepdims=True)
    water = jnp.broadcast_to(damping * (level + 1e-6), (8 * n, 128))
    slot = lax.broadcasted_iota(jnp.int32, (8 * n, 8 * n), 1)
    chip = ((slot // 8) % (chips // 4)) * 4 + (slot // (2 * chips)) % 4
    ids = chip * 16 + (slot // (8 * chips)) * 8 + slot % 8
    pick = jnp.where(wanted == ids.astype(jnp.float32), 1.0, 0.0).astype(jnp.float32)
    taps[...] = jnp.dot(pick, every, precision=HIGHEST, preferred_element_type=jnp.float32).reshape(n, 8, 256)
    floors[...] = jnp.dot(pick, water, precision=HIGHEST, preferred_element_type=jnp.float32).reshape(n, 8, 128)

    def block(k, _):
        @pl.when(k > 0)
        def _():
            raw_copy(k).wait_recv()

        sz, sc = source(k)
        p = place_of(sz, sc)
        deconvolve(raw.at[k], o_ref.at[sz * 2 + sc], taps.at[p], floors.at[p], across, twist, part, lhs, spec)
        return 0

    lax.fori_loop(0, n, block, 0)

    def finish(k, _):
        raw_copy(k).wait_send()
        return 0

    lax.fori_loop(1, n, finish, 0)


def exchange(n, x, index, damp, wave, across, twist):
    rows, length = x.shape
    hbm = pl.BlockSpec(memory_space=pltpu.HBM)
    smem = pl.BlockSpec(memory_space=pltpu.SMEM)
    f32 = jnp.float32
    dma = pltpu.SemaphoreType.DMA
    return pl.pallas_call(
        functools.partial(exchange_kernel, n),
        out_shape=jax.ShapeDtypeStruct((n, 8 * PITCH, 128), f32),
        in_specs=[hbm, smem, smem, pl.BlockSpec(memory_space=pltpu.VMEM), hbm, hbm],
        out_specs=pl.BlockSpec(memory_space=pltpu.VMEM),
        scratch_shapes=[
            pltpu.VMEM((n, 8, length), f32),
            pltpu.VMEM((n, 1, 128), f32),
            pltpu.VMEM((n, 1, 128), f32),
            pltpu.VMEM((2, 4, n // 8, 8, 256), f32),
            pltpu.VMEM((n, 8, 256), f32),
            pltpu.VMEM((n, 8, 128), f32),
            pltpu.VMEM(across.shape, f32),
            pltpu.VMEM(twist.shape, f32),
            pltpu.VMEM((8, 8, 8, 128), f32),
            pltpu.VMEM((2 * NK, 8, 256), f32),
            pltpu.VMEM((2 * NK, 8, 256), f32),
            dma((n,)), dma((n,)), dma((n,)), dma((n,)), dma((n // 8,)), dma((n // 8,)), dma((4,)), dma((4,)), dma((2,)),
            dma, dma((2,)),
        ],
        compiler_params=pltpu.CompilerParams(collective_id=0, has_side_effects=True, vmem_limit_bytes=VMEM_LIMIT),
    )(*(pltpu.with_memory_space_constraint(a, pltpu.HBM) for a in (x, index, damp, wave, across, twist)))


def reorder_kernel(n, order_ref, x_ref, o_ref, held, lined, out_sem):
    rows = o_ref.shape[0]
    tiles = rows // 8

    def out_copy(t):
        here = pl.ds(pl.multiple_of(t * 8, 8), 8)
        return pltpu.make_async_copy(lined.at[here], o_ref.at[here], out_sem.at[t])

    def line_up(t, _):
        for i in range(8):
            p = order_ref[t * 8 + i]
            held[pl.ds(i * PITCH, 64), :] = x_ref[p % n, pl.ds((p // n) * PITCH, 64), :]
        here = pl.ds(pl.multiple_of(t * 8, 8), 8)
        for i in range(64):
            lined[here, pl.ds(i * 128, 128)] = held[pl.ds(i, 8, stride=PITCH), :]
        out_copy(t).start()
        return 0

    lax.fori_loop(0, tiles, line_up, 0)

    def finish(t, _):
        out_copy(t).wait()
        return 0

    lax.fori_loop(0, tiles, finish, 0)


def reorder(n, order, x):
    rows, length = order.shape[0], 8192
    return pl.pallas_call(
        functools.partial(reorder_kernel, n),
        out_shape=jax.ShapeDtypeStruct((rows, length), x.dtype),
        in_specs=[pl.BlockSpec(memory_space=pltpu.SMEM), pl.BlockSpec(memory_space=pltpu.VMEM)],
        out_specs=pl.BlockSpec(memory_space=pl.ANY),
        scratch_shapes=[
            pltpu.VMEM((8 * PITCH, 128), x.dtype),
            pltpu.VMEM((rows, length), x.dtype),
            pltpu.SemaphoreType.DMA((rows // 8,)),
        ],
        compiler_params=pltpu.CompilerParams(vmem_limit_bytes=VMEM_LIMIT),
    )(pltpu.with_memory_space_constraint(order, pltpu.HBM), x)


def solution(mesh):
    n = mesh.shape["traces"]
    across, twist = tables()

    def local(raw_traces, filter_index, channel_order, wavelets, damping):
        moved = exchange(n, raw_traces, filter_index, damping, wavelets, jnp.asarray(across), jnp.asarray(twist))
        return reorder(n, channel_order, moved)

    placed = (
        P(("groups", "traces"), None),
        P(("groups", "traces")),
        P("groups"),
        P("traces", None),
        P("traces"),
    )
    return jax.shard_map(
        local, mesh=mesh, in_specs=placed, out_specs=P(("groups", "traces"), None), check_vma=False
    )
```

time: 704 us -> 392 us (0.56); the launches traced: 691 us -> 392 us
  Pallas kernels: 0 us -> 392 us
  waiting for transfers between devices: 391 us -> 0 us
  matrix products: 197 us -> 0 us
  local copies, waits for them, and re-layouts: 69.7 us -> 0 us
  between operations: 14.1 us -> 0.01 us
  starting transfers between devices: 10.1 us -> 0 us
  other arithmetic: 9.91 us -> 0 us
    pallas_call x0 -> x2, Pallas kernels: none -> 392 us  [the longest x1 387 us: exchange(): pl.pallas_call(functools.partial(exchange_kernel, n), out_shape=jax.Shape...]
    all_to_all x1 -> x0, waiting for transfers between devices: 360 us -> none  [local(): lax.all_to_all(stacked, 'traces', split_axis=0, concat_axis=2, tiled=True)]
    dot_general x18 -> x0, matrix products: 197 us -> none  [the longest x2 39.3 us: forward_spectra(): jnp.einsum('tkq,qm->tkm', mid_re, sin_q, precision=HIGHEST)]
    all_gather x1 -> x0, waiting for transfers between devices: 30.7 us -> none  [in_one_piece(): lax.all_gather(both, axis, axis=dim, tiled=True)]
    gather x3 -> x0, local copies, waits for them, and re-layouts: 28.8 us -> none  [the longest x1 13.2 us: local(): return jnp.take(ordered, channel_order, axis=0)]
    all_to_all x1 -> x0, local copies, waits for them, and re-layouts: 11.6 us -> none  [local(): lax.all_to_all(stacked, 'traces', split_axis=0, concat_axis=2, tiled=True)]
    slice x1 -> x0, local copies, waits for them, and re-layouts: 11 us -> none  [in_one_piece(): gathered.append(lax.slice_in_dim(out, at, at + a.shape[along], axis=along))]
    all_to_all x1 -> x0, starting transfers between devices: 10.1 us -> none  [local(): lax.all_to_all(stacked, 'traces', split_axis=0, concat_axis=2, tiled=True)]
  transfers between devices with their start and end apart: 2 -> 0, of which waited for: 2 -> 0; matrix products, arithmetic and copies ran while one was open for 11% -> 0% of each run, Pallas kernels for 0% -> 0%
where the time goes in v1:
time: 392 us
  Pallas kernels  392 us (100%)
    pallas_call x1, Pallas kernels, exchange(): pl.pallas_call(functools.partial(exchange_kernel, n), out_shape=jax.Shape...  387 us

profile of v1, /device:TPU:69, one launch (start us, length us, event | category | flops | bytes accessed | tf_op | source)
XLA Modules:
  0.0 391.5 jit_solution(13142743465242824564)
XLA Ops:
  0.0 387.2 %shard_map.73.x_ref = f32[32,520,128]{2,1,0:T(8,128)S(1)} custom-call(f32[256,8192]{1,0:T(8,128)} %x_ref.1, s32[256]{0:T(256)} %index_ref.1, f32[8]{0:T(128)} %damp_ref.1, f32[8,256]{1,0:T(8,128)} %wave_ref.1, f32[256,256]{1,0:T(8,128)} %constant.4.clone.across_ref, f32[4,33,8,128]{3,2,1,0:T(8,128)} %constant.5.clone.twist_ref), custom_call_target="tpu_custom_call" | custom-call | tf_op jit(solution)/shard_map/pallas_call | solution.py:351
  387.2 4.3 %shard_map.74 = f32[256,8192]{1,0:T(8,128)} custom-call(s32[256]{0:T(256)} %order_ref.1, f32[32,520,128]{2,1,0:T(8,128)S(1)} %shard_map.73.x_ref), custom_call_target="tpu_custom_call" | custom-call | tf_op jit(solution)/shard_map/pallas_call | solution.py:404

commit v2 on v1

--- a/solution.py
+++ b/solution.py
@@ -18,6 +18,7 @@
 CHUNK = 11
 PITCH = 65
 VMEM_LIMIT = 34 * 2**20
+LATE = 8
 
 
 def tables():
@@ -216,6 +217,15 @@
             device_id={"traces": t}, device_id_type=MESH,
         )
 
+    def late_copy(k):
+        return pltpu.make_async_remote_copy(
+            src_ref=o_ref.at[k + LATE], dst_ref=o_ref.at[me], send_sem=send.at[k], recv_sem=recv.at[k],
+            device_id={"traces": target(k)}, device_id_type=MESH,
+        )
+
+    def late_input(k):
+        return pltpu.make_async_copy(x_ref.at[eight_rows(target(k))], raw.at[k], own_sem.at[k - (n - LATE)])
+
     def note_copy(k):
         t = target(k)
         return pltpu.make_async_remote_copy(
@@ -242,19 +252,52 @@
             device_id={"traces": z * 2 + 1 - core}, device_id_type=MESH,
         )
 
+    away = [(chips // 2, 0), (chips // 2, 1)]
+    for d in range(chips // 2 - 1, 0, -1):
+        away += [(d, 0), (-d, 0), (d, 1), (-d, 1)]
+    away.append((0, 1))
+    cores = (core, 1 - core)
     barrier = pltpu.get_barrier_semaphore()
-
-    def greet(k, _):
-        pl.semaphore_signal(barrier, inc=1, device_id={"traces": target(k)}, device_id_type=MESH)
-        return 0
-
-    lax.fori_loop(1, n, greet, 0)
-    own_copy = pltpu.make_async_copy(x_ref.at[eight_rows(me)], raw.at[0], own_sem)
+    for dz, dc in away:
+        there = lax.rem(z + (dz + chips), chips) * 2 + cores[dc]
+        pl.semaphore_signal(barrier, inc=1, device_id={"traces": there}, device_id_type=MESH)
+    pl.semaphore_wait(barrier, n - 1)
+
+    def start_note(k, _):
+        note_copy(k).start()
+        return 0
+
+    def start_raw(k, _):
+        raw_copy(k).start()
+        return 0
+
+    def start_late(k, _):
+        late_copy(k).start()
+        return 0
+
+    def start_input(k, _):
+        late_input(k).start()
+        return 0
+
+    def wait_note(k, _):
+        note_copy(k).wait()
+        return 0
+
+    def wait_input(k, _):
+        late_input(k).wait()
+        return 0
+
+    for j in range(1, chips // 4):
+        wave_copy(j).start()
+    for k in (4, 5):
+        raw_copy(k).start()
+    own_copy = pltpu.make_async_copy(x_ref.at[eight_rows(me)], raw.at[0], own_sem.at[LATE])
     own_copy.start()
     across_copy = pltpu.make_async_copy(across_ref, across, table_sem.at[0])
     across_copy.start()
     twist_copy = pltpu.make_async_copy(twist_ref, twist, table_sem.at[1])
     twist_copy.start()
+    lax.fori_loop(n - LATE, n, start_input, 0)
     bank[core, z % 4, z // 4] = wave_ref[...]
     lane = lax.broadcasted_iota(jnp.int32, (1, 128), 1)
     damp = jnp.zeros((1, 128), jnp.float32)
@@ -270,76 +313,72 @@
 
     lax.fori_loop(0, n, fill, 0)
     note[mine] = own[me]
-    pl.semaphore_wait(barrier, n - 1)
-
-    def start_note(k, _):
-        note_copy(k).start()
-        return 0
-
-    def start_wave(j, _):
-        wave_copy(j).start()
-        return 0
-
-    def start_raw(k, _):
-        raw_copy(k).start()
-        return 0
-
-    def wait_wave(j, _):
+    for j in range(1, chips // 4):
         wave_copy(j).wait()
-        return 0
-
-    def wait_note(k, _):
-        note_copy(k).wait()
-        return 0
-
-    lax.fori_loop(1, chips // 4, start_wave, 0)
+    for j in (1, 2, 3):
+        fours_copy(j).start()
     lax.fori_loop(1, n, start_note, 0)
-    lax.fori_loop(1, 8, start_raw, 0)
+    lax.fori_loop(1, 4, start_raw, 0)
+    lax.fori_loop(6, n - LATE, start_raw, 0)
     own_copy.wait()
     across_copy.wait()
     twist_copy.wait()
-    lax.fori_loop(1, chips // 4, wait_wave, 0)
-    for j in (1, 2, 3):
-        fours_copy(j).start()
-    lax.fori_loop(8, n, start_raw, 0)
+    lax.fori_loop(n - LATE, n, wait_input, 0)
     for j in (1, 2, 3):
         fours_copy(j).wait()
     pass_copy().start()
     lax.fori_loop(1, n, wait_note, 0)
     pass_copy().wait()
 
-    notes = note[...]
     lanes = lax.broadcasted_iota(jnp.int32, (n, 8, 128), 2)
     place = lax.broadcasted_iota(jnp.int32, (n, 8, 128), 1)
-    wanted = jnp.sum(jnp.where(lanes == place, notes, 0.0), axis=2, keepdims=True).reshape(8 * n, 1)
-    damping = jnp.sum(jnp.where(lanes == place + 8, notes, 0.0), axis=2, keepdims=True).reshape(8 * n, 1)
+
+    def spread(notes, at):
+        return jnp.sum(jnp.where(lanes == place + at, notes, 0.0), axis=2, keepdims=True).reshape(8 * n, 1)
+
+    damping = spread(note[...], 8)
     every = bank[...].reshape(8 * n, 256)
     level = jnp.sum(every * every, axis=1, keepdims=True)
     water = jnp.broadcast_to(damping * (level + 1e-6), (8 * n, 128))
     slot = lax.broadcasted_iota(jnp.int32, (8 * n, 8 * n), 1)
     chip = ((slot // 8) % (chips // 4)) * 4 + (slot // (2 * chips)) % 4
     ids = chip * 16 + (slot // (8 * chips)) * 8 + slot % 8
-    pick = jnp.where(wanted == ids.astype(jnp.float32), 1.0, 0.0).astype(jnp.float32)
-    taps[...] = jnp.dot(pick, every, precision=HIGHEST, preferred_element_type=jnp.float32).reshape(n, 8, 256)
-    floors[...] = jnp.dot(pick, water, precision=HIGHEST, preferred_element_type=jnp.float32).reshape(n, 8, 128)
-
-    def block(k, _):
-        @pl.when(k > 0)
+    for half, notes in enumerate((note, own)):
+        pick = jnp.where(spread(notes[...], 0) == ids.astype(jnp.float32), 1.0, 0.0).astype(jnp.float32)
+        here = pl.ds(half * n, n)
+        taps[here] = jnp.dot(pick, every, precision=HIGHEST, preferred_element_type=jnp.float32).reshape(n, 8, 256)
+        floors[here] = jnp.dot(pick, water, precision=HIGHEST, preferred_element_type=jnp.float32).reshape(n, 8, 128)
+
+    def block(i, _):
+        k = (i + n - LATE) % n
+        raws = (i + n - LATE) // n
+        sz, sc = source(k)
+
+        @pl.when(i > LATE)
         def _():
             raw_copy(k).wait_recv()
 
-        sz, sc = source(k)
-        p = place_of(sz, sc)
-        deconvolve(raw.at[k], o_ref.at[sz * 2 + sc], taps.at[p], floors.at[p], across, twist, part, lhs, spec)
+        @pl.when(i == LATE + 1)
+        def _():
+            lax.fori_loop(n - LATE, n, start_late, 0)
+
+        out = raws * (sz * 2 + sc) + (1 - raws) * (n + i)
+        p = raws * place_of(sz, sc) + (1 - raws) * (n + target(k))
+        deconvolve(raw.at[k], o_ref.at[out], taps.at[p], floors.at[p], across, twist, part, lhs, spec)
         return 0
 
     lax.fori_loop(0, n, block, 0)
 
-    def finish(k, _):
+    def finish_raw(k, _):
         raw_copy(k).wait_send()
         return 0
 
-    lax.fori_loop(1, n, finish, 0)
+    def finish_late(k, _):
+        late_copy(k).wait()
+        return 0
+
+    lax.fori_loop(1, n - LATE, finish_raw, 0)
+    lax.fori_loop(n - LATE, n, finish_late, 0)
 
 
 def exchange(n, x, index, damp, wave, across, twist):
@@ -350,7 +389,7 @@
     dma = pltpu.SemaphoreType.DMA
     return pl.pallas_call(
         functools.partial(exchange_kernel, n),
-        out_shape=jax.ShapeDtypeStruct((n, 8 * PITCH, 128), f32),
+        out_shape=jax.ShapeDtypeStruct((n + LATE, 8 * PITCH, 128), f32),
         in_specs=[hbm, smem, smem, pl.BlockSpec(memory_space=pltpu.VMEM), hbm, hbm],
         out_specs=pl.BlockSpec(memory_space=pltpu.VMEM),
         scratch_shapes=[
@@ -358,21 +397,22 @@
             pltpu.VMEM((n, 1, 128), f32),
             pltpu.VMEM((n, 1, 128), f32),
             pltpu.VMEM((2, 4, n // 8, 8, 256), f32),
-            pltpu.VMEM((n, 8, 256), f32),
-            pltpu.VMEM((n, 8, 128), f32),
+            pltpu.VMEM((2 * n, 8, 256), f32),
+            pltpu.VMEM((2 * n, 8, 128), f32),
             pltpu.VMEM(across.shape, f32),
             pltpu.VMEM(twist.shape, f32),
             pltpu.VMEM((8, 8, 8, 128), f32),
             pltpu.VMEM((2 * NK, 8, 256), f32),
             pltpu.VMEM((2 * NK, 8, 256), f32),
             dma((n,)), dma((n,)), dma((n,)), dma((n,)), dma((n // 8,)), dma((n // 8,)), dma((4,)), dma((4,)), dma((2,)),
-            dma, dma((2,)),
+            dma((LATE + 1,)), dma((2,)),
         ],
         compiler_params=pltpu.CompilerParams(collective_id=0, has_side_effects=True, vmem_limit_bytes=VMEM_LIMIT),
     )(*(pltpu.with_memory_space_constraint(a, pltpu.HBM) for a in (x, index, damp, wave, across, twist)))
 
 
-def reorder_kernel(n, order_ref, x_ref, o_ref, held, lined, out_sem):
+def reorder_kernel(n, order_ref, x_ref, o_ref, *scratch):
+    *helds, lined, out_sem = scratch
     rows = o_ref.shape[0]
     tiles = rows // 8
 
@@ -380,17 +420,21 @@
         here = pl.ds(pl.multiple_of(t * 8, 8), 8)
         return pltpu.make_async_copy(lined.at[here], o_ref.at[here], out_sem.at[t])
 
-    def line_up(t, _):
-        for i in range(8):
-            p = order_ref[t * 8 + i]
-            held[pl.ds(i * PITCH, 64), :] = x_ref[p % n, pl.ds((p // n) * PITCH, 64), :]
-        here = pl.ds(pl.multiple_of(t * 8, 8), 8)
-        for i in range(64):
-            lined[here, pl.ds(i * 128, 128)] = held[pl.ds(i, 8, stride=PITCH), :]
-        out_copy(t).start()
-        return 0
-
-    lax.fori_loop(0, tiles, line_up, 0)
+    def line_up(g, _):
+        for u, held in enumerate(helds):
+            t = g * len(helds) + u
+            for i in range(8):
+                p = order_ref[t * 8 + i]
+                held[pl.ds(i * PITCH, 64), :] = x_ref[p % n, pl.ds((p // n) * PITCH, 64), :]
+        for u, held in enumerate(helds):
+            t = g * len(helds) + u
+            here = pl.ds(pl.multiple_of(t * 8, 8), 8)
+            for i in range(64):
+                lined[here, pl.ds(i * 128, 128)] = held[pl.ds(i, 8, stride=PITCH), :]
+            out_copy(t).start()
+        return 0
+
+    lax.fori_loop(0, tiles // len(helds), line_up, 0)
 
     def finish(t, _):
         out_copy(t).wait()
@@ -407,7 +451,7 @@
         in_specs=[pl.BlockSpec(memory_space=pltpu.SMEM), pl.BlockSpec(memory_space=pltpu.VMEM)],
         out_specs=pl.BlockSpec(memory_space=pl.ANY),
         scratch_shapes=[
-            pltpu.VMEM((8 * PITCH, 128), x.dtype),
+            *[pltpu.VMEM((8 * PITCH, 128), x.dtype)] * 4,
             pltpu.VMEM((rows, length), x.dtype),
             pltpu.SemaphoreType.DMA((rows // 8,)),
         ],

time: 392 us -> 389 us (level)
  no operation moved by 1% of the time
where the time goes in v2:
time: 389 us
  Pallas kernels  389 us (100%)
    pallas_call x1, Pallas kernels, exchange(): pl.pallas_call(functools.partial(exchange_kernel, n), out_shape=jax.Shape...  385 us

profile of v2, /device:TPU:69, one launch (start us, length us, event | category | flops | bytes accessed | tf_op | source)
XLA Modules:
  0.0 389.0 jit_solution(15805796473424537551)
XLA Ops:
  0.0 384.5 %shard_map.73.x_ref = f32[40,520,128]{2,1,0:T(8,128)S(1)} custom-call(f32[256,8192]{1,0:T(8,128)} %x_ref.1, s32[256]{0:T(256)} %index_ref.1, f32[8]{0:T(128)} %damp_ref.1, f32[8,256]{1,0:T(8,128)} %wave_ref.1, f32[256,256]{1,0:T(8,128)} %constant.4.clone.across_ref, f32[4,33,8,128]{3,2,1,0:T(8,128)} %constant.5.clone.twist_ref), custom_call_target="tpu_custom_call" | custom-call | tf_op jit(solution)/shard_map/pallas_call | solution.py:390
  384.5 4.5 %shard_map.74 = f32[256,8192]{1,0:T(8,128)} custom-call(s32[256]{0:T(256)} %order_ref.1, f32[40,520,128]{2,1,0:T(8,128)S(1)} %shard_map.73.x_ref), custom_call_target="tpu_custom_call" | custom-call | tf_op jit(solution)/shard_map/pallas_call | solution.py:448

commit v3 on v2

--- a/solution.py
+++ b/solution.py
@@ -182,7 +182,7 @@
     x_ref, index_ref, damp_ref, wave_ref, across_ref, twist_ref,
     o_ref,
     raw, own, note, bank, taps, floors, across, twist, part, lhs, spec,
-    send, recv, note_send, note_recv, wave_send, wave_recv, fours_send, fours_recv, pass_sem, own_sem, table_sem,
+    send, recv, note_send, note_recv, wave_send, wave_recv, fours_send, fours_recv, pass_sem, own_sem, table_sem, word,
 ):
     me = lax.axis_index("traces")
     chips = n // 2
@@ -194,9 +194,14 @@
     mine = place_of(z, core)
 
     def offset(k):
-        later = (k + n - 4) // n
-        dz = later * ((chips // 2 - k // 4) * (1 - 2 * (k % 2))) + (1 - later) * (chips // 2) * (k // 2)
-        dc = later * ((k // 2) % 2) + (1 - later) * (k % 2)
+        far = (k + n - 8) // n
+        m = k // 2
+        sign = 1 - 2 * (k % 2)
+        near_dz = (m + 1) // 2 + (chips // 2 - 2) * (m // 3)
+        one = ((m + 1) // 2) % 2
+        near_dc = one * (m // 2) + (1 - one) * (k % 2)
+        dz = sign * (far * (chips // 2 + 1 - k // 4) + (1 - far) * near_dz)
+        dc = far * (m % 2) + (1 - far) * near_dc
         return dz, dc
 
     def target(k):
@@ -252,16 +257,31 @@
             device_id={"traces": z * 2 + 1 - core}, device_id_type=MESH,
         )
 
-    away = [(chips // 2, 0), (chips // 2, 1)]
-    for d in range(chips // 2 - 1, 0, -1):
-        away += [(d, 0), (-d, 0), (d, 1), (-d, 1)]
-    away.append((0, 1))
-    cores = (core, 1 - core)
+    right = lax.rem(z + 1, chips) * 2
+    left = lax.rem(z + (chips - 1), chips) * 2
     barrier = pltpu.get_barrier_semaphore()
-    for dz, dc in away:
-        there = lax.rem(z + (dz + chips), chips) * 2 + cores[dc]
+    for there in (right + core, left + core, right + 1 - core, left + 1 - core, z * 2 + 1 - core):
         pl.semaphore_signal(barrier, inc=1, device_id={"traces": there}, device_id_type=MESH)
-    pl.semaphore_wait(barrier, n - 1)
+    pl.semaphore_wait(barrier, 5)
+
+    def tell(side):
+        there = (right if side == 0 else left) + core
+        pl.semaphore_signal(word.at[side], inc=1, device_id={"traces": there}, device_id_type=MESH)
+
+    tell(0)
+    tell(1)
+    for k in (2, 3, 4, 5, 1):
+        raw_copy(k).start()
+
+    def hear(_, __):
+        for side in (0, 1):
+            pl.semaphore_wait(word.at[side], 1)
+            tell(side)
+        return 0
+
+    lax.fori_loop(0, chips // 2 - 2, hear, 0)
+    for side in (0, 1):
+        pl.semaphore_wait(word.at[side], 1)
 
     def start_note(k, _):
         note_copy(k).start()
@@ -289,7 +309,7 @@
 
     for j in range(1, chips // 4):
         wave_copy(j).start()
-    for k in (4, 5):
+    for k in (8, 9):
         raw_copy(k).start()
     own_copy = pltpu.make_async_copy(x_ref.at[eight_rows(me)], raw.at[0], own_sem.at[LATE])
     own_copy.start()
@@ -318,8 +338,8 @@
     for j in (1, 2, 3):
         fours_copy(j).start()
     lax.fori_loop(1, n, start_note, 0)
-    lax.fori_loop(1, 4, start_raw, 0)
-    lax.fori_loop(6, n - LATE, start_raw, 0)
+    lax.fori_loop(6, 8, start_raw, 0)
+    lax.fori_loop(10, n - LATE, start_raw, 0)
     own_copy.wait()
     across_copy.wait()
     twist_copy.wait()
@@ -405,7 +425,7 @@
             pltpu.VMEM((2 * NK, 8, 256), f32),
             pltpu.VMEM((2 * NK, 8, 256), f32),
             dma((n,)), dma((n,)), dma((n,)), dma((n,)), dma((n // 8,)), dma((n // 8,)), dma((4,)), dma((4,)), dma((2,)),
-            dma((LATE + 1,)), dma((2,)),
+            dma((LATE + 1,)), dma((2,)), pltpu.SemaphoreType.REGULAR((2,)),
         ],
         compiler_params=pltpu.CompilerParams(collective_id=0, has_side_effects=True, vmem_limit_bytes=VMEM_LIMIT),
     )(*(pltpu.with_memory_space_constraint(a, pltpu.HBM) for a in (x, index, damp, wave, across, twist)))

time: 389 us -> 386 us (level)
  Pallas kernels: 389 us -> 384 us
    pallas_call x1, Pallas kernels: 385 us -> 379 us  [exchange(): pl.pallas_call(functools.partial(exchange_kernel, n), out_shape=jax.Shape...]
where the time goes in v3:
time: 386 us; the launch traced here: 384 us
  Pallas kernels  384 us (99%)
    pallas_call x1, Pallas kernels, exchange(): pl.pallas_call(functools.partial(exchange_kernel, n), out_shape=jax.Shape...  379 us

profile of v3, /device:TPU:69, one launch (start us, length us, event | category | flops | bytes accessed | tf_op | source)
XLA Modules:
  0.0 383.6 jit_solution(3594648948792687208)
XLA Ops:
  0.0 379.2 %shard_map.73.x_ref = f32[40,520,128]{2,1,0:T(8,128)S(1)} custom-call(f32[256,8192]{1,0:T(8,128)} %x_ref.1, s32[256]{0:T(256)} %index_ref.1, f32[8]{0:T(128)} %damp_ref.1, f32[8,256]{1,0:T(8,128)} %wave_ref.1, f32[256,256]{1,0:T(8,128)} %constant.4.clone.across_ref, f32[4,33,8,128]{3,2,1,0:T(8,128)} %constant.5.clone.twist_ref), custom_call_target="tpu_custom_call" | custom-call | tf_op jit(solution)/shard_map/pallas_call | solution.py:410
  379.2 4.5 %shard_map.74 = f32[256,8192]{1,0:T(8,128)} custom-call(s32[256]{0:T(256)} %order_ref.1, f32[40,520,128]{2,1,0:T(8,128)S(1)} %shard_map.73.x_ref), custom_call_target="tpu_custom_call" | custom-call | tf_op jit(solution)/shard_map/pallas_call | solution.py:468

commit v4 on v3

--- a/solution.py
+++ b/solution.py
@@ -179,14 +179,16 @@
 
 def exchange_kernel(
     n,
-    x_ref, index_ref, damp_ref, wave_ref, across_ref, twist_ref,
+    x_ref, index_hbm, damp_hbm, wave_ref, across_ref, twist_ref,
     o_ref,
-    raw, own, note, bank, taps, floors, across, twist, part, lhs, spec,
+    index_ref, damp_ref, raw, own, note, bank, taps, floors, across, twist, part, lhs, spec,
     send, recv, note_send, note_recv, wave_send, wave_recv, fours_send, fours_recv, pass_sem, own_sem, table_sem, word,
 ):
     me = lax.axis_index("traces")
     chips = n // 2
     z, core = me // 2, me % 2
+    group = lax.axis_index("groups")
+    half = group % 2
 
     def place_of(z, core):
         return core * chips + (z % 4) * (chips // 4) + z // 4
@@ -238,23 +240,32 @@
             device_id={"traces": t}, device_id_type=MESH,
         )
 
+    own_taps = wave_ref.at[:, pl.ds(pl.multiple_of(half * 128, 128), 128)]
+
     def wave_copy(j):
         return pltpu.make_async_remote_copy(
-            src_ref=wave_ref, dst_ref=bank.at[core, z % 4, z // 4], send_sem=wave_send.at[j], recv_sem=wave_recv.at[j],
+            src_ref=own_taps, dst_ref=bank.at[half, core, z % 4, z // 4], send_sem=wave_send.at[j], recv_sem=wave_recv.at[j],
             device_id={"traces": ((z + 4 * j) % chips) * 2 + core}, device_id_type=MESH,
         )
 
     def fours_copy(j):
         away = (0, 1, 2, chips - 1)[j]
-        return pltpu.make_async_remote_copy(
-            src_ref=bank.at[core, z % 4], dst_ref=bank.at[core, z % 4], send_sem=fours_send.at[j], recv_sem=fours_recv.at[j],
+        here = bank.at[half, core, z % 4]
+        return pltpu.make_async_remote_copy(
+            src_ref=here, dst_ref=here, send_sem=fours_send.at[j], recv_sem=fours_recv.at[j],
             device_id={"traces": ((z + away) % chips) * 2 + core}, device_id_type=MESH,
         )
 
     def pass_copy():
         return pltpu.make_async_remote_copy(
-            src_ref=bank.at[core], dst_ref=bank.at[core], send_sem=pass_sem.at[0], recv_sem=pass_sem.at[1],
+            src_ref=bank.at[half, core], dst_ref=bank.at[half, core], send_sem=pass_sem.at[0], recv_sem=pass_sem.at[1],
             device_id={"traces": z * 2 + 1 - core}, device_id_type=MESH,
+        )
+
+    def cross_copy():
+        return pltpu.make_async_remote_copy(
+            src_ref=bank.at[half], dst_ref=bank.at[half], send_sem=pass_sem.at[2], recv_sem=pass_sem.at[3],
+            device_id={"groups": group + 1 - 2 * half, "traces": me}, device_id_type=MESH,
         )
 
     right = lax.rem(z + 1, chips) * 2
@@ -262,7 +273,9 @@
     barrier = pltpu.get_barrier_semaphore()
     for there in (right + core, left + core, right + 1 - core, left + 1 - core, z * 2 + 1 - core):
         pl.semaphore_signal(barrier, inc=1, device_id={"traces": there}, device_id_type=MESH)
-    pl.semaphore_wait(barrier, 5)
+    other = {"groups": group + 1 - 2 * half, "traces": me}
+    pl.semaphore_signal(barrier, inc=1, device_id=other, device_id_type=MESH)
+    pl.semaphore_wait(barrier, 6)
 
     def tell(side):
         there = (right if side == 0 else left) + core
@@ -272,6 +285,13 @@
     tell(1)
     for k in (2, 3, 4, 5, 1):
         raw_copy(k).start()
+    small = [
+        pltpu.make_async_copy(index_hbm, index_ref, table_sem.at[2]),
+        pltpu.make_async_copy(damp_hbm, damp_ref, table_sem.at[3]),
+        pltpu.make_async_copy(own_taps, bank.at[half, core, z % 4, z // 4], table_sem.at[4]),
+    ]
+    for copy in small:
+        copy.start()
 
     def hear(_, __):
         for side in (0, 1):
@@ -318,7 +338,8 @@
     twist_copy = pltpu.make_async_copy(twist_ref, twist, table_sem.at[1])
     twist_copy.start()
     lax.fori_loop(n - LATE, n, start_input, 0)
-    bank[core, z % 4, z // 4] = wave_ref[...]
+    for copy in small:
+        copy.wait()
     lane = lax.broadcasted_iota(jnp.int32, (1, 128), 1)
     damp = jnp.zeros((1, 128), jnp.float32)
     for i in range(8):
@@ -349,6 +370,8 @@
     pass_copy().start()
     lax.fori_loop(1, n, wait_note, 0)
     pass_copy().wait()
+    cross_copy().start()
+    cross_copy().wait()
 
     lanes = lax.broadcasted_iota(jnp.int32, (n, 8, 128), 2)
     place = lax.broadcasted_iota(jnp.int32, (n, 8, 128), 1)
@@ -357,7 +380,7 @@
         return jnp.sum(jnp.where(lanes == place + at, notes, 0.0), axis=2, keepdims=True).reshape(8 * n, 1)
 
     damping = spread(note[...], 8)
-    every = bank[...].reshape(8 * n, 256)
+    every = jnp.concatenate([bank[0].reshape(8 * n, 128), bank[1].reshape(8 * n, 128)], axis=1)
     level = jnp.sum(every * every, axis=1, keepdims=True)
     water = jnp.broadcast_to(damping * (level + 1e-6), (8 * n, 128))
     slot = lax.broadcasted_iota(jnp.int32, (8 * n, 8 * n), 1)
@@ -404,19 +427,20 @@
 def exchange(n, x, index, damp, wave, across, twist):
     rows, length = x.shape
     hbm = pl.BlockSpec(memory_space=pltpu.HBM)
-    smem = pl.BlockSpec(memory_space=pltpu.SMEM)
     f32 = jnp.float32
     dma = pltpu.SemaphoreType.DMA
     return pl.pallas_call(
         functools.partial(exchange_kernel, n),
         out_shape=jax.ShapeDtypeStruct((n + LATE, 8 * PITCH, 128), f32),
-        in_specs=[hbm, smem, smem, pl.BlockSpec(memory_space=pltpu.VMEM), hbm, hbm],
+        in_specs=[hbm] * 6,
         out_specs=pl.BlockSpec(memory_space=pltpu.VMEM),
         scratch_shapes=[
+            pltpu.SMEM(index.shape, jnp.int32),
+            pltpu.SMEM(damp.shape, f32),
             pltpu.VMEM((n, 8, length), f32),
             pltpu.VMEM((n, 1, 128), f32),
             pltpu.VMEM((n, 1, 128), f32),
-            pltpu.VMEM((2, 4, n // 8, 8, 256), f32),
+            pltpu.VMEM((2, 2, 4, n // 8, 8, 128), f32),
             pltpu.VMEM((2 * n, 8, 256), f32),
             pltpu.VMEM((2 * n, 8, 128), f32),
             pltpu.VMEM(across.shape, f32),
@@ -424,8 +448,8 @@
             pltpu.VMEM((8, 8, 8, 128), f32),
             pltpu.VMEM((2 * NK, 8, 256), f32),
             pltpu.VMEM((2 * NK, 8, 256), f32),
-            dma((n,)), dma((n,)), dma((n,)), dma((n,)), dma((n // 8,)), dma((n // 8,)), dma((4,)), dma((4,)), dma((2,)),
-            dma((LATE + 1,)), dma((2,)), pltpu.SemaphoreType.REGULAR((2,)),
+            dma((n,)), dma((n,)), dma((n,)), dma((n,)), dma((n // 8,)), dma((n // 8,)), dma((4,)), dma((4,)), dma((4,)),
+            dma((LATE + 1,)), dma((5,)), pltpu.SemaphoreType.REGULAR((2,)),
         ],
         compiler_params=pltpu.CompilerParams(collective_id=0, has_side_effects=True, vmem_limit_bytes=VMEM_LIMIT),
     )(*(pltpu.with_memory_space_constraint(a, pltpu.HBM) for a in (x, index, damp, wave, across, twist)))
@@ -476,7 +500,7 @@
             pltpu.SemaphoreType.DMA((rows // 8,)),
         ],
         compiler_params=pltpu.CompilerParams(vmem_limit_bytes=VMEM_LIMIT),
-    )(pltpu.with_memory_space_constraint(order, pltpu.HBM), x)
+    )(order, x)
 
 
 def solution(mesh):

time: 386 us -> 383 us (level)
  no operation moved by 1% of the time
where the time goes in v4:
time: 383 us; the launch traced here: 382 us
  Pallas kernels  382 us (100%)
    pallas_call x1, Pallas kernels, exchange(): pl.pallas_call(functools.partial(exchange_kernel, n), out_shape=jax.Shape...  377 us

profile of v4, /device:TPU:69, one launch (start us, length us, event | category | flops | bytes accessed | tf_op | source)
XLA Modules:
  0.0 381.7 jit_solution(12241696309374926891)
XLA Ops:
  0.0 0.0 copy-start
  0.0 377.3 %shard_map.73.x_ref = f32[40,520,128]{2,1,0:T(8,128)S(1)} custom-call(f32[256,8192]{1,0:T(8,128)} %x_ref.1, s32[256]{0:T(256)} %index_hbm.1, f32[8]{0:T(128)} %damp_hbm.1, f32[8,256]{1,0:T(8,128)} %wave_ref.1, f32[256,256]{1,0:T(8,128)} %constant.4.clone.across_ref, f32[4,33,8,128]{3,2,1,0:T(8,128)} %constant.5.clone.twist_ref), custom_call_target="tpu_custom_call" | custom-call | tf_op jit(solution)/shard_map/pallas_call | solution.py:432
  377.3 0.0 copy-done
  377.4 4.3 %shard_map.74 = f32[256,8192]{1,0:T(8,128)} custom-call(s32[256]{0:T(256)S(1)} %copy-done, f32[40,520,128]{2,1,0:T(8,128)S(1)} %shard_map.73.x_ref), custom_call_target="tpu_custom_call" | custom-call | tf_op jit(solution)/shard_map/pallas_call | solution.py:492
Async XLA Ops:
  0.0 377.3 %copy-start = (s32[256]{0:T(256)S(1)}, s32[256]{0:T(256)}, u32[]{:S(2)}) copy-start(s32[256]{0:T(256)} %order_ref.1) | copy-start | bytes 3076

commit v5 on v4

--- a/solution.py
+++ b/solution.py
@@ -224,9 +224,10 @@
             device_id={"traces": t}, device_id_type=MESH,
         )
 
-    def late_copy(k):
-        return pltpu.make_async_remote_copy(
-            src_ref=o_ref.at[k + LATE], dst_ref=o_ref.at[me], send_sem=send.at[k], recv_sem=recv.at[k],
+    def late_copy(k, at, size):
+        here = pl.ds(at, size)
+        return pltpu.make_async_remote_copy(
+            src_ref=o_ref.at[k + LATE, here], dst_ref=o_ref.at[me, here], send_sem=send.at[k], recv_sem=recv.at[k],
             device_id={"traces": target(k)}, device_id_type=MESH,
         )
 
@@ -312,7 +313,8 @@
         return 0
 
     def start_late(k, _):
-        late_copy(k).start()
+        for i in range(8):
+            late_copy(k, i * PITCH, 64).start()
         return 0
 
     def start_input(k, _):
@@ -417,7 +419,7 @@
         return 0
 
     def finish_late(k, _):
-        late_copy(k).wait()
+        late_copy(k, 0, 512).wait()
         return 0
 
     lax.fori_loop(1, n - LATE, finish_raw, 0)
@@ -462,7 +464,7 @@
 
     def out_copy(t):
         here = pl.ds(pl.multiple_of(t * 8, 8), 8)
-        return pltpu.make_async_copy(lined.at[here], o_ref.at[here], out_sem.at[t])
+        return pltpu.make_async_copy(lined.at[here], o_ref.at[here], out_sem)
 
     def line_up(g, _):
         for u, held in enumerate(helds):
@@ -480,11 +482,7 @@
 
     lax.fori_loop(0, tiles // len(helds), line_up, 0)
 
-    def finish(t, _):
-        out_copy(t).wait()
-        return 0
-
-    lax.fori_loop(0, tiles, finish, 0)
+    pltpu.make_async_copy(lined, o_ref, out_sem).wait()
 
 
 def reorder(n, order, x):
@@ -497,7 +495,7 @@
         scratch_shapes=[
             *[pltpu.VMEM((8 * PITCH, 128), x.dtype)] * 4,
             pltpu.VMEM((rows, length), x.dtype),
-            pltpu.SemaphoreType.DMA((rows // 8,)),
+            pltpu.SemaphoreType.DMA,
         ],
         compiler_params=pltpu.CompilerParams(vmem_limit_bytes=VMEM_LIMIT),
     )(order, x)

time: 383 us -> 382 us (level)
  no operation moved by 1% of the time
where the time goes in v5:
time: 382 us; the launch traced here: 381 us
  Pallas kernels  380 us (99%)
    pallas_call x1, Pallas kernels, exchange(): pl.pallas_call(functools.partial(exchange_kernel, n), out_shape=jax.Shape...  376 us

profile of v5, /device:TPU:69, one launch (start us, length us, event | category | flops | bytes accessed | tf_op | source)
XLA Modules:
  0.0 380.5 jit_solution(17997344824891847921)
XLA Ops:
  0.0 0.0 copy-start
  0.0 376.5 %shard_map.73.x_ref = f32[40,520,128]{2,1,0:T(8,128)S(1)} custom-call(f32[256,8192]{1,0:T(8,128)} %x_ref.1, s32[256]{0:T(256)} %index_hbm.1, f32[8]{0:T(128)} %damp_hbm.1, f32[8,256]{1,0:T(8,128)} %wave_ref.1, f32[256,256]{1,0:T(8,128)} %constant.4.clone.across_ref, f32[4,33,8,128]{3,2,1,0:T(8,128)} %constant.5.clone.twist_ref), custom_call_target="tpu_custom_call" | custom-call | tf_op jit(solution)/shard_map/pallas_call | solution.py:434
  376.5 0.0 copy-done
  376.5 4.0 %shard_map.74 = f32[256,8192]{1,0:T(8,128)} custom-call(s32[256]{0:T(256)S(1)} %copy-done, f32[40,520,128]{2,1,0:T(8,128)S(1)} %shard_map.73.x_ref), custom_call_target="tpu_custom_call" | custom-call | tf_op jit(solution)/shard_map/pallas_call | solution.py:490
Async XLA Ops:
  0.0 376.5 %copy-start = (s32[256]{0:T(256)S(1)}, s32[256]{0:T(256)}, u32[]{:S(2)}) copy-start(s32[256]{0:T(256)} %order_ref.1) | copy-start | bytes 3076

commit v6 on v5

--- a/solution.py
+++ b/solution.py
@@ -188,7 +188,8 @@
     chips = n // 2
     z, core = me // 2, me % 2
     group = lax.axis_index("groups")
-    half = group % 2
+    half, pair = group % 2, (group // 2) % 2
+    four = pl.ds(pl.multiple_of(pair * 4, 4), 4)
 
     def place_of(z, core):
         return core * chips + (z % 4) * (chips // 4) + z // 4
@@ -241,17 +242,17 @@
             device_id={"traces": t}, device_id_type=MESH,
         )
 
-    own_taps = wave_ref.at[:, pl.ds(pl.multiple_of(half * 128, 128), 128)]
+    own_taps = wave_ref.at[four, pl.ds(pl.multiple_of(half * 128, 128), 128)]
 
     def wave_copy(j):
         return pltpu.make_async_remote_copy(
-            src_ref=own_taps, dst_ref=bank.at[half, core, z % 4, z // 4], send_sem=wave_send.at[j], recv_sem=wave_recv.at[j],
+            src_ref=own_taps, dst_ref=bank.at[half, core, z % 4, z // 4, four], send_sem=wave_send.at[j], recv_sem=wave_recv.at[j],
             device_id={"traces": ((z + 4 * j) % chips) * 2 + core}, device_id_type=MESH,
         )
 
     def fours_copy(j):
         away = (0, 1, 2, chips - 1)[j]
-        here = bank.at[half, core, z % 4]
+        here = bank.at[half, core, z % 4, :, four]
         return pltpu.make_async_remote_copy(
             src_ref=here, dst_ref=here, send_sem=fours_send.at[j], recv_sem=fours_recv.at[j],
             device_id={"traces": ((z + away) % chips) * 2 + core}, device_id_type=MESH,
@@ -259,14 +260,23 @@
 
     def pass_copy():
         return pltpu.make_async_remote_copy(
-            src_ref=bank.at[half, core], dst_ref=bank.at[half, core], send_sem=pass_sem.at[0], recv_sem=pass_sem.at[1],
+            src_ref=bank.at[half, core, :, :, four], dst_ref=bank.at[half, core, :, :, four], send_sem=pass_sem.at[0], recv_sem=pass_sem.at[1],
             device_id={"traces": z * 2 + 1 - core}, device_id_type=MESH,
         )
 
+    other = {"groups": group + 1 - 2 * half, "traces": me}
+    far_other = {"groups": group + 2 - 4 * pair, "traces": me}
+
     def cross_copy():
         return pltpu.make_async_remote_copy(
-            src_ref=bank.at[half], dst_ref=bank.at[half], send_sem=pass_sem.at[2], recv_sem=pass_sem.at[3],
-            device_id={"groups": group + 1 - 2 * half, "traces": me}, device_id_type=MESH,
+            src_ref=bank.at[half, :, :, :, four], dst_ref=bank.at[half, :, :, :, four],
+            send_sem=pass_sem.at[2], recv_sem=pass_sem.at[3], device_id=other, device_id_type=MESH,
+        )
+
+    def far_cross_copy():
+        return pltpu.make_async_remote_copy(
+            src_ref=bank.at[:, :, :, :, four], dst_ref=bank.at[:, :, :, :, four],
+            send_sem=pass_sem.at[4], recv_sem=pass_sem.at[5], device_id=far_other, device_id_type=MESH,
         )
 
     right = lax.rem(z + 1, chips) * 2
@@ -274,9 +284,9 @@
     barrier = pltpu.get_barrier_semaphore()
     for there in (right + core, left + core, right + 1 - core, left + 1 - core, z * 2 + 1 - core):
         pl.semaphore_signal(barrier, inc=1, device_id={"traces": there}, device_id_type=MESH)
-    other = {"groups": group + 1 - 2 * half, "traces": me}
-    pl.semaphore_signal(barrier, inc=1, device_id=other, device_id_type=MESH)
-    pl.semaphore_wait(barrier, 6)
+    for there in (other, far_other):
+        pl.semaphore_signal(barrier, inc=1, device_id=there, device_id_type=MESH)
+    pl.semaphore_wait(barrier, 7)
 
     def tell(side):
         there = (right if side == 0 else left) + core
@@ -289,7 +299,7 @@
     small = [
         pltpu.make_async_copy(index_hbm, index_ref, table_sem.at[2]),
         pltpu.make_async_copy(damp_hbm, damp_ref, table_sem.at[3]),
-        pltpu.make_async_copy(own_taps, bank.at[half, core, z % 4, z // 4], table_sem.at[4]),
+        pltpu.make_async_copy(own_taps, bank.at[half, core, z % 4, z // 4, four], table_sem.at[4]),
     ]
     for copy in small:
         copy.start()
@@ -374,6 +384,8 @@
     pass_copy().wait()
     cross_copy().start()
     cross_copy().wait()
+    far_cross_copy().start()
+    far_cross_copy().wait()
 
     lanes = lax.broadcasted_iota(jnp.int32, (n, 8, 128), 2)
     place = lax.broadcasted_iota(jnp.int32, (n, 8, 128), 1)
@@ -450,7 +462,7 @@
             pltpu.VMEM((8, 8, 8, 128), f32),
             pltpu.VMEM((2 * NK, 8, 256), f32),
             pltpu.VMEM((2 * NK, 8, 256), f32),
-            dma((n,)), dma((n,)), dma((n,)), dma((n,)), dma((n // 8,)), dma((n // 8,)), dma((4,)), dma((4,)), dma((4,)),
+            dma((n,)), dma((n,)), dma((n,)), dma((n,)), dma((n // 8,)), dma((n // 8,)), dma((4,)), dma((4,)), dma((6,)),
             dma((LATE + 1,)), dma((5,)), pltpu.SemaphoreType.REGULAR((2,)),
         ],
         compiler_params=pltpu.CompilerParams(collective_id=0, has_side_effects=True, vmem_limit_bytes=VMEM_LIMIT),

time: 382 us -> 381 us (level)
  no operation moved by 1% of the time
where the time goes in v6:
time: 381 us; the launch traced here: 380 us
  Pallas kernels  380 us (100%)
    pallas_call x1, Pallas kernels, exchange(): pl.pallas_call(functools.partial(exchange_kernel, n), out_shape=jax.Shape...  376 us

profile of v6, /device:TPU:69, one launch (start us, length us, event | category | flops | bytes accessed | tf_op | source)
XLA Modules:
  0.0 380.0 jit_solution(9771898031046794133)
XLA Ops:
  0.0 0.0 copy-start
  0.0 375.9 %shard_map.73.x_ref = f32[40,520,128]{2,1,0:T(8,128)S(1)} custom-call(f32[256,8192]{1,0:T(8,128)} %x_ref.1, s32[256]{0:T(256)} %index_hbm.1, f32[8]{0:T(128)} %damp_hbm.1, f32[8,256]{1,0:T(8,128)} %wave_ref.1, f32[256,256]{1,0:T(8,128)} %constant.4.clone.across_ref, f32[4,33,8,128]{3,2,1,0:T(8,128)} %constant.5.clone.twist_ref), custom_call_target="tpu_custom_call" | custom-call | tf_op jit(solution)/shard_map/pallas_call | solution.py:446
  376.0 0.0 copy-done
  376.0 4.0 %shard_map.74 = f32[256,8192]{1,0:T(8,128)} custom-call(s32[256]{0:T(256)S(1)} %copy-done, f32[40,520,128]{2,1,0:T(8,128)S(1)} %shard_map.73.x_ref), custom_call_target="tpu_custom_call" | custom-call | tf_op jit(solution)/shard_map/pallas_call | solution.py:502
Async XLA Ops:
  0.0 376.0 %copy-start = (s32[256]{0:T(256)S(1)}, s32[256]{0:T(256)}, u32[]{:S(2)}) copy-start(s32[256]{0:T(256)} %order_ref.1) | copy-start | bytes 3076
